TPU v7x, 32 devices: a whole 2x2x4 slice. The times are simulated.
32 devices in a mesh: dp: 8 (over z, y), owner: 4 (over x, core).
Axes of the slice: x: 2, y: 2, z: 4, core: 2. Of those that a mesh axis runs over, the one named last changes fastest.
Arguments:
- gradients: bfloat16 [8, 4, 512, 512], P('dp', 'owner'), may hold values from -600 to 600
- block_layer: int32 [4], P('owner'), may hold values from 0 to 3
Outputs:
- update: bfloat16 [4, 512, 512], P('owner', 'dp')
All inputs are finite; a program needn't handle non-finite values.
Results may differ from a plain program's by a relative error of at most 0.0062.
Values may be sent and summed in bfloat16 or wider, within the bound.
A program may use at most 64 MiB of HBM per device.

v0:
```python
import jax
import jax.numpy as jnp
from jax import lax
from jax.sharding import PartitionSpec as P

LAYERS = 4
ITERS = 3


def from_partner(x, axis, distance):
    return lax.ppermute(x, axis, [(i, i ^ 1 << distance) for i in range(lax.axis_size(axis))])


def own_whole(partial_rows, position, members):
    gathered = partial_rows
    for bit_number in range(members.bit_length() - 1):
        partner = from_partner(gathered, "dp", bit_number)
        upper_half = position // (1 << bit_number) % 2 == 1
        gathered = jnp.where(
            upper_half,
            jnp.concatenate([partner, gathered], axis=0),
            jnp.concatenate([gathered, partner], axis=0),
        )
    return gathered


def keep_whole(partial_rows):
    return partial_rows


def root_slab(stat_rows, eye_rows, assemble):
    size_b = stat_rows.shape[1]
    identity = jnp.eye(size_b, dtype=jnp.float32)
    statistic = assemble(stat_rows)
    ridge_term = 0.01 * jnp.trace(statistic) / size_b + 1e-06
    shifted_whole = statistic + ridge_term * identity
    scaling = jnp.sqrt(jnp.sum(shifted_whole * shifted_whole))
    current_whole = shifted_whole / scaling
    current_rows = (stat_rows + ridge_term * eye_rows) / scaling
    inverse_rows = eye_rows
    for step_number in range(ITERS):
        factor_whole = (5.0 * identity - current_whole) / 4.0
        factor_rows = (5.0 * eye_rows - current_rows) / 4.0
        if step_number == 0:
            inverse_rows = scaling ** (-0.25) * factor_rows
        else:
            inverse_rows = jnp.dot(inverse_rows, factor_whole, precision=lax.Precision.HIGHEST)
        if step_number + 1 < ITERS:
            square_rows = jnp.dot(factor_rows, factor_whole, precision=lax.Precision.HIGHEST)
            square_whole = assemble(square_rows)
            fourth_rows = jnp.dot(square_rows, square_whole, precision=lax.Precision.HIGHEST)
            current_rows = jnp.dot(fourth_rows, current_whole, precision=lax.Precision.HIGHEST)
            current_whole = assemble(current_rows)
    return inverse_rows


def per_device(gradients, block_layer):
    gradient = gradients[0, 0]
    size_b = gradient.shape[0]
    dp_count = lax.axis_size("dp")
    members = dp_count // 2
    height = size_b // members
    position = lax.axis_index("dp")
    offset = position % members * height
    left_gram = lax.dot_general(
        gradient, gradient, (((1,), (1,)), ((), ())), preferred_element_type=jnp.float32
    )
    right_gram = lax.dot_general(
        gradient, gradient, (((0,), (0,)), ((), ())), preferred_element_type=jnp.float32
    )
    stacked = jnp.concatenate([left_gram, right_gram], axis=0)
    half_rows = lax.psum_scatter(stacked, "dp", scatter_dimension=0, tiled=True)
    statistic = own_whole(half_rows, position, members)
    inverse_whole = root_slab(statistic, jnp.eye(size_b, dtype=jnp.float32), keep_whole)
    inverse_rows = lax.dynamic_slice_in_dim(inverse_whole, offset, height, 0)
    both_roots = lax.all_gather(inverse_rows.astype(jnp.bfloat16), "dp", axis=0, tiled=True)
    left_root = both_roots[:size_b]
    right_root = both_roots[size_b:]
    out_height = size_b // dp_count
    right_wide = right_root.astype(jnp.float32)
    left_part = lax.slice_in_dim(left_root, 0, out_height * lax.axis_size("dp"), axis=0)
    middle = jnp.dot(left_part, gradient, preferred_element_type=jnp.float32)
    summed = lax.psum_scatter(
        jnp.dot(middle, right_wide, precision=lax.Precision.HIGHEST),
        "dp",
        scatter_dimension=0,
        tiled=True,
    )
    precond = summed / dp_count
    layer_id = block_layer[0]
    selector = (jnp.arange(LAYERS, dtype=jnp.int32) == layer_id).astype(jnp.float32)
    energy = jnp.sum(precond * precond)
    totals_sq, counts = lax.psum(
        (selector * energy, selector * float(precond.size)), ("dp", "owner")
    )
    mean_square = jnp.sum(selector * totals_sq) / jnp.sum(selector * counts)
    update = (precond * lax.rsqrt(mean_square + 1e-06)).astype(jnp.bfloat16)
    return update[None]


def solution(mesh):
    return jax.shard_map(
        per_device,
        mesh=mesh,
        in_specs=(P("dp", "owner", None, None), P("owner")),
        out_specs=P("owner", "dp", None),
        check_vma=False,
    )
```

profile of v0, /device:TPU:0, one launch (start us, length us, event | category | flops | bytes accessed | tf_op | source)
XLA Modules:
  0.0 283.0 jit_solution(12800960964047001834)
XLA Ops:
  6.5 0.0 copy-start
  6.5 0.0 reduce-scatter.3.cloned.1.call-start
  6.5 1.0 copy-done
  7.6 0.5 fusion.15
  8.0 0.5 fusion.17
  8.5 1.5 pad_maximum_fusion
  10.0 0.0 reduce-scatter.3.cloned.1.call-update
  10.1 0.0 all-gather.2.cloned.1.call-start
  10.1 72.2 %reduce-scatter.3.cloned.1.call-done = f32[128,512]{1,0:T(8,128)} async-done(((f32[1024,512]{1,0:T(8,128)}), f32[128,512]{1,0:T(8,128)}) %reduce-scatter.3.cloned.1.call-update) | async-done | bytes 262160 | tf_op jit(solution)/shard_map/reduce_scatter | solution.py:72
  82.3 0.5 collective-permute-start
  82.9 6.2 %collective-permute-done = f32[128,512]{1,0:T(8,128)S(1)} collective-permute-done((f32[128,512]{1,0:T(8,128)}, f32[128,512]{1,0:T(8,128)S(1)}, u32[]{:S(2)}, u32[]{:S(2)}) %collective-permute-start) | collective-permute-done | bytes 262176 | tf_op jit(solution)/shard_map/ppermute | solution.py:11
  89.1 1.1 maximum_select_fusion.1
  90.2 1.1 collective-permute-start.1
  91.3 10.2 %collective-permute-done.1 = f32[256,512]{1,0:T(8,128)S(1)} collective-permute-done((f32[256,512]{1,0:T(8,128)S(1)}, f32[256,512]{1,0:T(8,128)S(1)}, u32[]{:S(2)}, u32[]{:S(2)}) %collective-permute-start.1) | collective-permute-done | bytes 524320 | tf_op jit(solution)/shard_map/ppermute | solution.py:11
  101.5 0.0 copy-start.1
  101.5 0.7 select_reduce_fusion
  102.8 0.9 multiply_reduce_fusion
  104.4 2.1 fusion.2
  106.5 2.8 %fusion.45 = f32[512,512]{1,0:T(8,128)} fusion(f32[512,512]{1,0:T(8,128)S(1)} %fusion.2), kind=kOutput, calls=%fused_computation.56 | convolution fusion | flops 1610612736 | bytes 2097152 | tf_op jit(solution)/shard_map/dot_general | solution.py:51
  109.4 0.0 copy-done.1
  109.4 3.2 %fusion.42 = f32[512,512]{1,0:T(8,128)S(1)} fusion(f32[512,512]{1,0:T(8,128)} %fusion.45, f32[]{:T(128)S(6)} %sqrt.3, f32[]{:T(128)S(6)} %add.35, f32[256,512]{1,0:T(8,128)S(1)} %collective-permute-done.1, f32[256,512]{1,0:T(8,128)S(1)} %maximum_select_fusion.1, pred[]{:T(512)S(6)} %eq.31), kind=kOutput, calls=%fused_computation.55 | convolution fusion | flops 1612447744 | bytes 3145737 | tf_op jit(solution)/shard_map/dot_general | solution.py:52
  112.6 1.9 fusion.7
  114.5 1.8 fusion.46
  116.3 1.9 fusion
  118.2 3.5 %fusion.4 = f32[512,512]{1,0:T(8,128)S(1)} fusion(f32[512,512]{1,0:T(8,128)S(1)} %fusion.42, f32[]{:T(128)S(6)} %mul.63, f32[]{:T(128)S(6)} %sqrt.3, f32[]{:T(128)S(6)} %add.35, f32[256,512]{1,0:T(8,128)} %copy-done.1, f32[256,512]{1,0:T(8,128)S(1)} %maximum_select_fusion.1, pred[]{:T(512)S(6)} %eq.31), kind=kOutput, calls=%fused_computation.9 | convolution fusion | flops 1614282752 | bytes 3145741 | tf_op jit(solution)/shard_map/dot_general | solution.py:47
  121.7 1.9 fusion.47
  123.5 0.7 dynamic-slice_convert_fusion
  124.2 0.0 all-gather.2.cloned.1.call-update
  124.2 0.0 reduce-scatter.5.cloned.1.call-start
  124.3 39.4 %all-gather.2.cloned.1.call-done = bf16[1024,512]{1,0:T(8,128)(2,1)} async-done(((bf16[128,512]{1,0:T(8,128)(2,1)}), bf16[1024,512]{1,0:T(8,128)(2,1)}) %all-gather.2.cloned.1.call-update) | async-done | bytes 1048592 | tf_op jit(solution)/shard_map/all_gather | solution.py:76
  163.7 0.0 copy-start.2
  163.7 1.6 fusion.12
  165.2 0.0 copy-done.2
  165.2 2.0 fusion.10
  167.2 0.0 reduce-scatter.5.cloned.1.call-update
  167.9 62.8 %reduce-scatter.5.cloned.1.call-done = f32[64,512]{1,0:T(8,128)} async-done(((f32[512,512]{1,0:T(8,128)}), f32[64,512]{1,0:T(8,128)}) %reduce-scatter.5.cloned.1.call-update) | async-done | bytes 131088 | tf_op jit(solution)/shard_map/reduce_scatter | solution.py:83
  230.7 1.5 multiply_reduce_fusion.1
  232.3 0.6 fusion.31
  232.9 39.9 %all-reduce = (f32[4]{0:T(128)S(1)}, f32[4]{0:T(128)S(1)}) all-reduce(f32[4]{0:T(128)S(1)} %fusion.31, f32[4]{0:T(128)S(1)} %fusion.30), channel_id=1, replica_groups=mesh['dp'=8,'owner'=4] {'dp','owner'}, use_global_device_ids=true, to_apply=%region_5.6 | all-reduce | flops 8 | bytes 64 | tf_op jit(solution)/shard_map/psum | solution.py:93
  272.8 0.7 select_reduce_fusion.1
  274.9 1.5 fusion.29
  (1 shorter events, 0.0 us)
Async XLA Ops:
  6.5 1.0 copy-start
  6.5 75.8 %reduce-scatter.3.cloned.1.call-start = ((), (), s32[]{:S(2)}) async-start(), calls=%async_computation.2 | async-start | bytes 2359296 | tf_op jit(solution)/shard_map/reduce_scatter | solution.py:72
  10.1 153.6 %all-gather.2.cloned.1.call-start = ((), (), s32[]{:S(2)}) async-start(), calls=%async_computation.3 | async-start | bytes 1179648 | tf_op jit(solution)/shard_map/all_gather | solution.py:76
  82.3 6.7 %collective-permute-start = (f32[128,512]{1,0:T(8,128)}, f32[128,512]{1,0:T(8,128)S(1)}, u32[]{:S(2)}, u32[]{:S(2)}) collective-permute-start(f32[128,512]{1,0:T(8,128)} %reduce-scatter.3.cloned.1.call-done), channel_id=1, source_target_pairs={{0,4},{4,0},{8,12},{12,8},{16,20},{20,16},{24,28},{28,24},{1,5},{5... | collective-permute-start | bytes 786440 | tf_op jit(solution)/shard_map/ppermute | solution.py:11
  90.2 11.3 %collective-permute-start.1 = (f32[256,512]{1,0:T(8,128)S(1)}, f32[256,512]{1,0:T(8,128)S(1)}, u32[]{:S(2)}, u32[]{:S(2)}) collective-permute-start(f32[256,512]{1,0:T(8,128)S(1)} %maximum_select_fusion.1), channel_id=1, source_target_pairs={{0,8},{4,12},{8,0},{12,4},{16,24},{20,28},{24,16},{28,20},{1,9},{5... | collective-permute-start | bytes 1572872 | tf_op jit(solution)/shard_map/ppermute | solution.py:11
  101.5 7.9 %copy-start.1 = (f32[256,512]{1,0:T(8,128)}, f32[256,512]{1,0:T(8,128)S(1)}, u32[]{:S(2)}) copy-start(f32[256,512]{1,0:T(8,128)S(1)} %collective-permute-done.1) | copy-start | bytes 1572868
  124.2 106.5 %reduce-scatter.5.cloned.1.call-start = ((), (), s32[]{:S(2)}) async-start(), calls=%async_computation.4 | async-start | bytes 1179648 | tf_op jit(solution)/shard_map/reduce_scatter | solution.py:83
  163.7 1.6 copy-start.2
Sparse Core Ops, SparseCore 0:
  10.9 71.4 reduce-scatter.2
  124.3 39.2 all-gather.1
  167.4 63.3 reduce-scatter.4
where the time goes:
time: 283 us
  waiting for transfers between devices  191 us (67%)
  blocking collectives  39.9 us (14%)
  matrix products  23.5 us (8%)
  between operations  16.7 us (6%)
  other arithmetic  8.61 us (3%)
    reduce_scatter x1, waiting for transfers between devices, per_device(): half_rows = lax.psum_scatter(stacked, 'dp', scatter_dimension=0, tiled=True)  72.2 us
    reduce_scatter x1, waiting for transfers between devices, per_device(): lax.psum_scatter(jnp.dot(middle, right_wide, precision=lax.Precision.HIGH...  62.8 us
    psum x1, blocking collectives, per_device(): lax.psum((selector * energy, selector * float(precond.size)), ('dp', 'own...  39.9 us
    all_gather x1, waiting for transfers between devices, per_device(): lax.all_gather(inverse_rows.astype(jnp.bfloat16), 'dp', axis=0, tiled=True)  39.4 us
    ppermute x2, waiting for transfers between devices, from_partner(): lax.ppermute(x, axis, [(i, i ^ 1 << distance) for i in range(lax.axis_siz...  16.4 us
  transfers between devices with their start and end apart: 5, of which 5 were waited for; matrix products, arithmetic and copies ran while one was open for 0% of the time, Pallas kernels for 0%

commit v1 on v0

v1 whole, which is shorter than its diff:
```python
import functools

import jax
import jax.numpy as jnp
from jax import lax
from jax.experimental import pallas as pl
from jax.experimental.pallas import tpu as pltpu
from jax.sharding import PartitionSpec as P

LAYERS = 4
ITERS = 3
TILE = 128
BF16 = jnp.bfloat16
F32 = jnp.float32
MESH = pl.DeviceIdType.MESH


def mm(a, b):
    return jnp.dot(a.astype(BF16), b.astype(BF16), preferred_element_type=F32)


def upper_tiles(size_b):
    t = size_b // TILE
    return [(i, j) for i in range(t) for j in range(i, t)]


def pack(gram, acc_ref, size_b):
    tiles = upper_tiles(size_b)
    for n, (i, j) in enumerate(tiles):
        block = gram[i * TILE:(i + 1) * TILE, j * TILE:(j + 1) * TILE]
        acc_ref[n * TILE:(n + 1) * TILE, :] = block.astype(BF16)
    used, rows = len(tiles) * TILE, acc_ref.shape[0]
    if rows > used:
        acc_ref[used:, :] = jnp.zeros((rows - used, TILE), BF16)


def unpack(gath_ref, stat_ref, size_b):
    for n, (i, j) in enumerate(upper_tiles(size_b)):
        block = gath_ref[n * TILE:(n + 1) * TILE, :].astype(F32)
        stat_ref[i * TILE:(i + 1) * TILE, j * TILE:(j + 1) * TILE] = block
        if i != j:
            stat_ref[j * TILE:(j + 1) * TILE, i * TILE:(i + 1) * TILE] = block.T


def inverse_root(stat_ref, size_b):
    rows = lax.broadcasted_iota(jnp.int32, (size_b, size_b), 0)
    cols = lax.broadcasted_iota(jnp.int32, (size_b, size_b), 1)
    diag = rows == cols
    stat = stat_ref[...]
    trace = jnp.sum(jnp.where(diag, stat, 0.0), keepdims=True)
    ridge = 0.01 * trace / size_b + 1e-06
    shifted = stat + jnp.where(diag, ridge, 0.0)
    norm2 = jnp.sum(shifted * shifted, keepdims=True)
    m = shifted * lax.rsqrt(norm2)
    a, y = 1.25, -0.25 * m
    for step in range(1, ITERS):
        square = mm(m, m)
        once = (25.0 * m - 10.0 * square + mm(m, square)) * 0.0625
        m = 1.5625 * once + mm((square - 10.0 * m) * 0.0625, once)
        y = 1.25 * y - (0.25 * a) * m - 0.25 * mm(y, m)
        a = 1.25 * a
    scale = lax.rsqrt(jnp.sqrt(jnp.sqrt(norm2)))
    return scale * (y + jnp.where(diag, a, 0.0))


class Piece:
    def __init__(self, index, me, order, acc, gath, landing, send, recv, target):
        self.index, self.me, self.order = index, me, order
        self.acc, self.gath, self.landing = acc, gath, landing
        self.send, self.recv, self.target = send, recv, target
        self.start_row, self.length = 0, acc.shape[0]
        self.copy, self.offset = None, 0

    def bit(self, number):
        d = 1 << number
        mine = self.me // d % 2
        return mine, self.me + d * (1 - 2 * mine)

    def rows(self, first, length):
        return pl.ds(pl.multiple_of(first, 16), length)

    def start(self, step):
        nb = len(self.order)
        if step < nb:
            mine, partner = self.bit(self.order[step])
            half = self.length // 2
            src = self.acc.at[self.rows(self.start_row + (1 - mine) * half, half)]
            dst = self.landing.at[pl.ds(self.offset, half)]
        else:
            mine, partner = self.bit(self.order[2 * nb - 1 - step])
            here = self.rows(self.start_row, self.length)
            src, dst = self.gath.at[here], self.gath.at[here]
        self.copy = pltpu.make_async_remote_copy(
            src_ref=src,
            dst_ref=dst,
            send_sem=self.send.at[self.index, step],
            recv_sem=self.recv.at[self.index, step],
            device_id=self.target(partner),
            device_id_type=MESH,
        )
        self.copy.start()

    def finish(self, step):
        nb = len(self.order)
        self.copy.wait()
        if step < nb:
            mine, _ = self.bit(self.order[step])
            half = self.length // 2
            first = self.start_row + mine * half
            keep = self.rows(first, half)
            arrived = self.landing[pl.ds(self.offset, half), :].astype(F32)
            total = (self.acc[keep, :].astype(F32) + arrived).astype(BF16)
            (self.acc if step + 1 < nb else self.gath)[keep, :] = total
            self.start_row, self.length = first, half
            self.offset += half
        else:
            mine, _ = self.bit(self.order[2 * nb - 1 - step])
            self.start_row = self.start_row - mine * self.length
            self.length *= 2


def kernel(dp_count, owners, layer_ref, g_ref, out_ref, acc_s, gath_s, land_s, acc_g, gath_g,
           land_g, stats, roots, precond, e_src, e_buf, send, recv, e_send, e_recv):
    me = lax.axis_index("dp")
    own = lax.axis_index("owner")
    size_b = g_ref.shape[0]
    nb = dp_count.bit_length() - 1

    barrier = pltpu.get_barrier_semaphore()
    for number in range(nb):
        d = 1 << number
        partner = me + d * (1 - 2 * (me // d % 2))
        pl.semaphore_signal(barrier, inc=1, device_id=(partner, own), device_id_type=MESH)
    for j in range(1, owners):
        pl.semaphore_signal(
            barrier, inc=1, device_id=(me, lax.rem(own + j, owners)), device_id_type=MESH
        )

    order_a = list(range(nb))
    order_b = order_a[1::-1] + order_a[2:]
    target = lambda partner: (partner, own)
    stat_pieces = [
        Piece(i, me, order, acc_s.at[i], gath_s.at[i], land_s.at[i], send, recv, target)
        for i, order in enumerate((order_a, order_b))
    ]
    grad_pieces = [
        Piece(2 + i, me, order, acc_g.at[i], gath_g.at[i], land_g.at[i], send, recv, target)
        for i, order in enumerate((order_a, order_b))
    ]
    g = g_ref[...]
    width = size_b // 2
    left = lax.dot_general(g, g, (((1,), (1,)), ((), ())), preferred_element_type=F32)
    pack(left, acc_s.at[0], size_b)
    pl.semaphore_wait(barrier, nb + owners - 1)
    stat_pieces[0].start(0)
    right = lax.dot_general(g, g, (((0,), (0,)), ((), ())), preferred_element_type=F32)
    pack(right, acc_s.at[1], size_b)
    stat_pieces[1].start(0)
    for i in range(2):
        acc_g[i] = g[:, i * width:(i + 1) * width]
        grad_pieces[i].start(0)

    steps = 2 * nb
    for step in range(steps):
        for piece in stat_pieces:
            piece.finish(step)
            if step + 1 < steps:
                piece.start(step + 1)
        if step + 1 < steps:
            for piece in grad_pieces:
                piece.finish(step)
                piece.start(step + 1)

    def solve(i, carry):
        unpack(gath_s.at[i], stats, size_b)
        roots[i] = inverse_root(stats, size_b).astype(BF16)
        return carry

    lax.fori_loop(0, 2, solve, 0)
    for piece in grad_pieces:
        piece.finish(steps - 1)

    for i in range(2):
        cols = slice(i * width, (i + 1) * width)
        stats[:, cols] = jnp.dot(roots[0], gath_g[i], preferred_element_type=F32)
    middle = stats[...]
    high = middle.astype(BF16)
    low = (middle - high.astype(F32)).astype(BF16)
    right_root = roots[1]
    whole = jnp.dot(high, right_root, preferred_element_type=F32)
    whole += jnp.dot(low, right_root, preferred_element_type=F32)
    whole = whole / dp_count
    precond[...] = whole
    energy = jnp.sum(whole * whole, keepdims=True)

    layer = layer_ref[0]
    sub = lax.broadcasted_iota(jnp.int32, e_src.shape, 0)
    lane = lax.broadcasted_iota(jnp.int32, e_src.shape, 1)
    mine = lane == layer
    value = jnp.where(sub == 0, energy, float(size_b * size_b))
    e_src[...] = jnp.where(mine, value, 0.0)
    copies = []
    for j in range(1, owners):
        copy = pltpu.make_async_remote_copy(
            src_ref=e_src,
            dst_ref=e_buf.at[j - 1],
            send_sem=e_send.at[j - 1],
            recv_sem=e_recv.at[j - 1],
            device_id=(me, lax.rem(own + j, owners)),
            device_id_type=MESH,
        )
        copy.start()
        copies.append(copy)
    totals = e_src[...]
    for j, copy in enumerate(copies):
        copy.wait()
        totals += e_buf[j]
    energies = jnp.sum(jnp.where(mine & (sub == 0), totals, 0.0), keepdims=True)
    counts = jnp.sum(jnp.where(mine & (sub == 1), totals, 0.0), keepdims=True)
    height = out_ref.shape[0]
    rows = precond[pl.ds(pl.multiple_of(me * height, 16), height), :]
    out_ref[...] = (rows * lax.rsqrt(energies / counts + 1e-06)).astype(BF16)


def per_device(dp_count, owners, gradients, block_layer):
    size_b = gradients.shape[-1]
    nb = dp_count.bit_length() - 1
    used = len(upper_tiles(size_b)) * TILE
    unit = 16 * dp_count
    packed = -(-used // unit) * unit
    height = size_b // dp_count
    width = size_b // 2
    out = pl.pallas_call(
        functools.partial(kernel, dp_count, owners),
        out_shape=jax.ShapeDtypeStruct((height, size_b), BF16),
        in_specs=[
            pl.BlockSpec(memory_space=pltpu.SMEM),
            pl.BlockSpec(memory_space=pltpu.VMEM),
        ],
        out_specs=pl.BlockSpec(memory_space=pltpu.VMEM),
        scratch_shapes=[
            pltpu.VMEM((2, packed, TILE), BF16),
            pltpu.VMEM((2, packed, TILE), BF16),
            pltpu.VMEM((2, packed, TILE), BF16),
            pltpu.VMEM((2, size_b, width), BF16),
            pltpu.VMEM((2, size_b, width), BF16),
            pltpu.VMEM((2, size_b, width), BF16),
            pltpu.VMEM((size_b, size_b), F32),
            pltpu.VMEM((2, size_b, size_b), BF16),
            pltpu.VMEM((size_b, size_b), F32),
            pltpu.VMEM((8, TILE), F32),
            pltpu.VMEM((owners - 1, 8, TILE), F32),
            pltpu.SemaphoreType.DMA((4, 2 * nb)),
            pltpu.SemaphoreType.DMA((4, 2 * nb)),
            pltpu.SemaphoreType.DMA((owners - 1,)),
            pltpu.SemaphoreType.DMA((owners - 1,)),
        ],
        compiler_params=pltpu.CompilerParams(
            collective_id=0, has_side_effects=True, vmem_limit_bytes=48 * 1024 * 1024
        ),
    )(block_layer, gradients[0, 0])
    return out[None]


def solution(mesh):
    return jax.shard_map(
        functools.partial(per_device, mesh.shape["dp"], mesh.shape["owner"]),
        mesh=mesh,
        in_specs=(P("dp", "owner", None, None), P("owner")),
        out_specs=P("owner", "dp", None),
        check_vma=False,
    )
```

time: 283 us -> 52.1 us (0.18)
  waiting for transfers between devices: 191 us -> 0 us
  Pallas kernels: 0 us -> 49.6 us
  blocking collectives: 39.9 us -> 0 us
  matrix products: 23.5 us -> 0 us
  between operations: 16.7 us -> 0.67 us
  other arithmetic: 8.61 us -> 0 us
    reduce_scatter x2 -> x0, waiting for transfers between devices: 135 us -> none  [the longest x1 72.2 us: per_device(): half_rows = lax.psum_scatter(stacked, 'dp', scatter_dimension=0, tiled=True)]
    pallas_call x0 -> x1, Pallas kernels: none -> 49.6 us  [per_device(): pl.pallas_call(functools.partial(kernel, dp_count, owners), out_shape=jax...]
    psum x1 -> x0, blocking collectives: 39.9 us -> none  [per_device(): lax.psum((selector * energy, selector * float(precond.size)), ('dp', 'own...]
    all_gather x1 -> x0, waiting for transfers between devices: 39.4 us -> none  [per_device(): lax.all_gather(inverse_rows.astype(jnp.bfloat16), 'dp', axis=0, tiled=True)]
    dot_general x12 -> x0, matrix products: 23.5 us -> none  [the longest x2 5.31 us: root_slab(): jnp.dot(inverse_rows, factor_whole, precision=lax.Precision.HIGHEST)]
    ppermute x2 -> x0, waiting for transfers between devices: 16.4 us -> none  [from_partner(): lax.ppermute(x, axis, [(i, i ^ 1 << distance) for i in range(lax.axis_siz...]
    reduce_sum x4 -> x0, other arithmetic: 3.8 us -> none  [the longest x1 1.54 us: per_device(): energy = jnp.sum(precond * precond)]
  transfers between devices with their start and end apart: 5 -> 0, of which waited for: 5 -> 0; matrix products, arithmetic and copies ran while one was open for 0% -> 0% of each run, Pallas kernels for 0% -> 0%
where the time goes in v1:
time: 52.1 us; the launch traced here: 52 us
  Pallas kernels  49.6 us (95%)
  local copies, waits for them, and re-layouts  1.67 us (3%)
  between operations  0.67 us (1%)
    pallas_call x1, Pallas kernels, per_device(): pl.pallas_call(functools.partial(kernel, dp_count, owners), out_shape=jax...  49.6 us
    unnamed x3, local copies, waits for them, and re-layouts  1.67 us

profile of v1, /device:TPU:0, one launch (start us, length us, event | category | flops | bytes accessed | tf_op | source)
XLA Modules:
  0.0 52.0 jit_solution(3603891412326645992)
XLA Ops:
  0.7 0.0 copy-start
  0.7 1.0 %copy-done = bf16[1,1,512,512]{3,2,1,0:T(8,128)(2,1)S(1)} copy-done((bf16[1,1,512,512]{3,2,1,0:T(8,128)(2,1)S(1)}, bf16[1,1,512,512]{3,2,1,0:T(8,128)(2,1)}, u32[]{:S(2)}) %copy-start) | copy-done | bytes 524312
  1.7 49.6 %shard_map.28 = bf16[64,512]{1,0:T(8,128)(2,1)S(1)} custom-call(s32[1]{0:T(128)S(6)} %copy.4.layer_ref, bf16[512,512]{1,0:T(8,128)(2,1)S(1)} %bitcast.2), custom_call_target="tpu_custom_call" | custom-call | tf_op jit(solution)/shard_map/pallas_call | solution.py:233
  51.3 0.6 %copy.5 = bf16[1,64,512]{2,1,0:T(8,128)(2,1)} copy(bf16[1,64,512]{2,1,0:T(8,128)(2,1)S(1)} %bitcast.3) | data formatting | bytes 131072
Async XLA Ops:
  0.7 1.0 %copy-start = (bf16[1,1,512,512]{3,2,1,0:T(8,128)(2,1)S(1)}, bf16[1,1,512,512]{3,2,1,0:T(8,128)(2,1)}, u32[]{:S(2)}) copy-start(bf16[1,1,512,512]{3,2,1,0:T(8,128)(2,1)} %param.2) | copy-start | bytes 1572868

commit v2 on v1

v2 whole, which is shorter than its diff:
```python
import functools

import jax
import jax.numpy as jnp
from jax import lax
from jax.experimental import pallas as pl
from jax.experimental.pallas import tpu as pltpu
from jax.sharding import PartitionSpec as P

LAYERS = 4
ITERS = 3
TILE = 128
LAG = 1
BF16 = jnp.bfloat16
F32 = jnp.float32
MESH = pl.DeviceIdType.MESH


def mm(a, b):
    return jnp.dot(a.astype(BF16), b.astype(BF16), preferred_element_type=F32)


def upper_tiles(size_b):
    t = size_b // TILE
    return [(i, j) for i in range(t) for j in range(i, t)]


def pack(gram, acc_ref, first, size_b):
    tiles = upper_tiles(size_b)
    per_piece = acc_ref.shape[1] // TILE
    for n, (i, j) in enumerate(tiles):
        block = gram[i * TILE:(i + 1) * TILE, j * TILE:(j + 1) * TILE]
        row = n % per_piece * TILE
        acc_ref[first + n // per_piece, row:row + TILE, :] = block.astype(BF16)
    for n in range(len(tiles), 2 * per_piece):
        row = n % per_piece * TILE
        acc_ref[first + n // per_piece, row:row + TILE, :] = jnp.zeros((TILE, TILE), BF16)


def unpack(gath_ref, first, stat_ref, size_b):
    per_piece = gath_ref.shape[1] // TILE
    for n, (i, j) in enumerate(upper_tiles(size_b)):
        row = n % per_piece * TILE
        block = gath_ref[first + n // per_piece, row:row + TILE, :].astype(F32)
        stat_ref[i * TILE:(i + 1) * TILE, j * TILE:(j + 1) * TILE] = block
        if i != j:
            stat_ref[j * TILE:(j + 1) * TILE, i * TILE:(i + 1) * TILE] = block.T


def inverse_root(gath_ref, first, stat_ref, root_ref, size_b):
    unpack(gath_ref, first, stat_ref, size_b)
    rows = lax.broadcasted_iota(jnp.int32, (size_b, size_b), 0)
    cols = lax.broadcasted_iota(jnp.int32, (size_b, size_b), 1)
    diag = rows == cols
    stat = stat_ref[...]
    trace = jnp.sum(jnp.where(diag, stat, 0.0), keepdims=True)
    ridge = 0.01 * trace / size_b + 1e-06
    shifted = stat + jnp.where(diag, ridge, 0.0)
    norm2 = jnp.sum(shifted * shifted, keepdims=True)
    m = shifted * lax.rsqrt(norm2)
    a, y = 1.25, -0.25 * m
    for step in range(1, ITERS):
        yield
        square = mm(m, m)
        once = (25.0 * m - 10.0 * square + mm(m, square)) * 0.0625
        yield
        m = 1.5625 * once + mm((square - 10.0 * m) * 0.0625, once)
        y = 1.25 * y - (0.25 * a) * m - 0.25 * mm(y, m)
        a = 1.25 * a
    scale = lax.rsqrt(jnp.sqrt(jnp.sqrt(norm2)))
    root_ref[...] = (scale * (y + jnp.where(diag, a, 0.0))).astype(BF16)


def label_bit(me, number):
    d = 1 << number
    mine = me // d % 2
    return mine, me + d * (1 - 2 * mine)


class Piece:
    def __init__(self, index, me, order, acc, gath, landing, send, recv, target):
        self.index, self.me, self.order = index, me, order
        self.acc, self.gath, self.landing = acc, gath, landing
        self.send, self.recv, self.target = send, recv, target
        self.start_row, self.length = 0, acc.shape[0]
        self.copy, self.offset = None, 0

    def bit(self, number):
        return label_bit(self.me, number)

    def rows(self, first, length):
        return pl.ds(pl.multiple_of(first, 16), length)

    def start(self, step):
        last = len(self.order) - 1
        mine, partner = self.bit(self.order[last - abs(last - step)])
        if step < last:
            half = self.length // 2
            src = self.acc.at[self.rows(self.start_row + (1 - mine) * half, half)]
            dst = self.landing.at[pl.ds(self.offset, half)]
        elif step == last:
            src = self.acc.at[self.rows(self.start_row, self.length)]
            dst = self.landing.at[pl.ds(self.offset, self.length)]
        else:
            here = self.rows(self.start_row, self.length)
            src, dst = self.gath.at[here], self.gath.at[here]
        self.copy = pltpu.make_async_remote_copy(
            src_ref=src,
            dst_ref=dst,
            send_sem=self.send.at[self.index, step],
            recv_sem=self.recv.at[self.index, step],
            device_id=self.target(partner),
            device_id_type=MESH,
        )
        self.copy.start()

    def finish(self, step):
        last = len(self.order) - 1
        mine, _ = self.bit(self.order[last - abs(last - step)])
        self.copy.wait()
        if step <= last:
            if step < last:
                self.length //= 2
                self.start_row = self.start_row + mine * self.length
            keep = self.rows(self.start_row, self.length)
            arrived = self.landing[pl.ds(self.offset, self.length), :].astype(F32)
            total = (self.acc[keep, :].astype(F32) + arrived).astype(BF16)
            (self.acc if step < last else self.gath)[keep, :] = total
            self.offset += self.length
        else:
            self.start_row = self.start_row - mine * self.length
            self.length *= 2


def kernel(dp_count, owners, layer_ref, g_ref, out_ref, acc_s, gath_s, land_s, acc_g, gath_g,
           land_g, stats, roots, middle, middle_rows, e_src, e_buf, send, recv, e_send, e_recv):
    me = lax.axis_index("dp")
    own = lax.axis_index("owner")
    size_b = g_ref.shape[0]
    nb = dp_count.bit_length() - 1

    barrier = pltpu.get_barrier_semaphore()
    for number in range(nb):
        _, partner = label_bit(me, number)
        pl.semaphore_signal(barrier, inc=1, device_id=(partner, own), device_id_type=MESH)
    for j in range(1, owners):
        pl.semaphore_signal(
            barrier, inc=1, device_id=(me, lax.rem(own + j, owners)), device_id_type=MESH
        )

    order_a = list(range(nb))
    order_b = order_a[1::-1] + order_a[2:]
    target = lambda partner: (partner, own)
    orders = (order_a, order_b)
    left_pieces, right_pieces = (
        [
            Piece(n, me, orders[n % 2], acc_s.at[n], gath_s.at[n], land_s.at[n], send, recv, target)
            for n in pair
        ]
        for pair in ((0, 1), (2, 3))
    )
    grad_pieces = [
        Piece(4 + n, me, orders[n], acc_g.at[n], gath_g.at[n], land_g.at[n], send, recv, target)
        for n in range(2)
    ]
    g = g_ref[...]
    width = size_b // 2
    left = lax.dot_general(g, g, (((1,), (1,)), ((), ())), preferred_element_type=F32)
    pack(left, acc_s, 0, size_b)
    pl.semaphore_wait(barrier, nb + owners - 1)
    for piece in left_pieces:
        piece.start(0)
    right = lax.dot_general(g, g, (((0,), (0,)), ((), ())), preferred_element_type=F32)
    pack(right, acc_s, 2, size_b)
    for piece in right_pieces:
        piece.start(0)
    for n, piece in enumerate(grad_pieces):
        acc_g[n] = g[:, n * width:(n + 1) * width]
        piece.start(0)

    steps = 2 * nb - 1
    left_solve = inverse_root(gath_s, 0, stats.at[0], roots.at[0], size_b)
    right_solve = inverse_root(gath_s, 2, stats.at[1], roots.at[1], size_b)

    def attend(pieces, step):
        for piece in pieces:
            piece.finish(step)
            if step + 1 < steps:
                piece.start(step + 1)

    solvers = []

    def advance():
        while solvers:
            try:
                next(solvers[0])
                return
            except StopIteration:
                solvers.pop(0)

    for turn in range(steps + LAG):
        if turn < steps:
            attend(left_pieces, turn)
            if turn + 1 == steps:
                solvers.append(left_solve)
                advance()
            attend(right_pieces, turn)
            if turn + 1 == steps:
                solvers.append(right_solve)
                advance()
        if 0 <= turn - LAG < steps:
            attend(grad_pieces, turn - LAG)
            advance()
    while solvers:
        advance()

    height = out_ref.shape[0]
    mine_rows = pl.ds(pl.multiple_of(me * height, 16), height)
    halves = [slice(n * width, (n + 1) * width) for n in range(2)]
    right_root = roots[1]
    for n in range(2):
        middle[:, halves[n]] = jnp.dot(
            roots[0], gath_g[n], preferred_element_type=F32
        ).astype(BF16)
        middle_rows[:, halves[n]] = jnp.dot(
            roots[0, mine_rows, :], gath_g[n], preferred_element_type=F32
        )
    whole = jnp.dot(middle[...], right_root, preferred_element_type=F32) / dp_count
    energy = jnp.sum(whole * whole, keepdims=True)

    layer = layer_ref[0]
    sub = lax.broadcasted_iota(jnp.int32, e_src.shape, 0)
    lane = lax.broadcasted_iota(jnp.int32, e_src.shape, 1)
    mine = lane == layer
    value = jnp.where(sub == 0, energy, float(size_b * size_b))
    e_src[...] = jnp.where(mine, value, 0.0)
    copies = []
    for j in range(1, owners):
        copy = pltpu.make_async_remote_copy(
            src_ref=e_src,
            dst_ref=e_buf.at[j - 1],
            send_sem=e_send.at[j - 1],
            recv_sem=e_recv.at[j - 1],
            device_id=(me, lax.rem(own + j, owners)),
            device_id_type=MESH,
        )
        copy.start()
        copies.append(copy)
    high = middle_rows[...].astype(BF16)
    low = (middle_rows[...] - high.astype(F32)).astype(BF16)
    rows = jnp.dot(high, right_root, preferred_element_type=F32)
    rows = (rows + jnp.dot(low, right_root, preferred_element_type=F32)) / dp_count
    totals = e_src[...]
    for j, copy in enumerate(copies):
        copy.wait()
        totals += e_buf[j]
    energies = jnp.sum(jnp.where(mine & (sub == 0), totals, 0.0), keepdims=True)
    counts = jnp.sum(jnp.where(mine & (sub == 1), totals, 0.0), keepdims=True)
    out_ref[...] = (rows * lax.rsqrt(energies / counts + 1e-06)).astype(BF16)


def per_device(dp_count, owners, gradients, block_layer):
    size_b = gradients.shape[-1]
    nb = dp_count.bit_length() - 1
    used = len(upper_tiles(size_b)) * TILE
    unit = max(32 * dp_count, 2 * TILE)
    packed = -(-used // unit) * unit
    height = size_b // dp_count
    width = size_b // 2
    out = pl.pallas_call(
        functools.partial(kernel, dp_count, owners),
        out_shape=jax.ShapeDtypeStruct((height, size_b), BF16),
        in_specs=[
            pl.BlockSpec(memory_space=pltpu.SMEM),
            pl.BlockSpec(memory_space=pltpu.VMEM),
        ],
        out_specs=pl.BlockSpec(memory_space=pltpu.VMEM),
        scratch_shapes=[
            pltpu.VMEM((4, packed // 2, TILE), BF16),
            pltpu.VMEM((4, packed // 2, TILE), BF16),
            pltpu.VMEM((4, packed // 2, TILE), BF16),
            pltpu.VMEM((2, size_b, width), BF16),
            pltpu.VMEM((2, size_b, width), BF16),
            pltpu.VMEM((2, size_b, width), BF16),
            pltpu.VMEM((2, size_b, size_b), F32),
            pltpu.VMEM((2, size_b, size_b), BF16),
            pltpu.VMEM((size_b, size_b), BF16),
            pltpu.VMEM((height, size_b), F32),
            pltpu.VMEM((8, TILE), F32),
            pltpu.VMEM((owners - 1, 8, TILE), F32),
            pltpu.SemaphoreType.DMA((6, 2 * nb - 1)),
            pltpu.SemaphoreType.DMA((6, 2 * nb - 1)),
            pltpu.SemaphoreType.DMA((owners - 1,)),
            pltpu.SemaphoreType.DMA((owners - 1,)),
        ],
        compiler_params=pltpu.CompilerParams(
            collective_id=0, has_side_effects=True, vmem_limit_bytes=48 * 1024 * 1024
        ),
    )(block_layer, gradients[0, 0])
    return out[None]


def solution(mesh):
    return jax.shard_map(
        functools.partial(per_device, mesh.shape["dp"], mesh.shape["owner"]),
        mesh=mesh,
        in_specs=(P("dp", "owner", None, None), P("owner")),
        out_specs=P("owner", "dp", None),
        check_vma=False,
    )
```

time: 52.1 us -> 47.8 us (0.917)
  Pallas kernels: 49.6 us -> 45.3 us
    pallas_call x1, Pallas kernels: 49.6 us -> 45.3 us  [per_device(): pl.pallas_call(functools.partial(kernel, dp_count, owners), out_shape=jax...]
where the time goes in v2:
time: 47.8 us; the launch traced here: 47.6 us
  Pallas kernels  45.3 us (95%)
  local copies, waits for them, and re-layouts  1.67 us (3%)
  between operations  0.67 us (1%)
    pallas_call x1, Pallas kernels, per_device(): pl.pallas_call(functools.partial(kernel, dp_count, owners), out_shape=jax...  45.3 us
    unnamed x3, local copies, waits for them, and re-layouts  1.67 us

profile of v2, /device:TPU:0, one launch (start us, length us, event | category | flops | bytes accessed | tf_op | source)
XLA Modules:
  0.0 47.6 jit_solution(4645978259434255442)
XLA Ops:
  0.7 0.0 copy-start
  0.7 1.0 %copy-done = bf16[1,1,512,512]{3,2,1,0:T(8,128)(2,1)S(1)} copy-done((bf16[1,1,512,512]{3,2,1,0:T(8,128)(2,1)S(1)}, bf16[1,1,512,512]{3,2,1,0:T(8,128)(2,1)}, u32[]{:S(2)}) %copy-start) | copy-done | bytes 524312
  1.7 45.3 %shard_map.28 = bf16[64,512]{1,0:T(8,128)(2,1)S(1)} custom-call(s32[1]{0:T(128)S(6)} %copy.4.layer_ref, bf16[512,512]{1,0:T(8,128)(2,1)S(1)} %bitcast.2), custom_call_target="tpu_custom_call" | custom-call | tf_op jit(solution)/shard_map/pallas_call | solution.py:270
  47.0 0.6 %copy.5 = bf16[1,64,512]{2,1,0:T(8,128)(2,1)} copy(bf16[1,64,512]{2,1,0:T(8,128)(2,1)S(1)} %bitcast.3) | data formatting | bytes 131072
Async XLA Ops:
  0.7 1.0 %copy-start = (bf16[1,1,512,512]{3,2,1,0:T(8,128)(2,1)S(1)}, bf16[1,1,512,512]{3,2,1,0:T(8,128)(2,1)}, u32[]{:S(2)}) copy-start(bf16[1,1,512,512]{3,2,1,0:T(8,128)(2,1)} %param.2) | copy-start | bytes 1572868

commit v3 on v2

--- a/solution.py
+++ b/solution.py
@@ -174,9 +174,8 @@
     pack(right, acc_s, 2, size_b)
     for piece in right_pieces:
         piece.start(0)
-    for n, piece in enumerate(grad_pieces):
+    for n in range(2):
         acc_g[n] = g[:, n * width:(n + 1) * width]
-        piece.start(0)
 
     steps = 2 * nb - 1
     left_solve = inverse_root(gath_s, 0, stats.at[0], roots.at[0], size_b)
@@ -208,6 +207,9 @@
             if turn + 1 == steps:
                 solvers.append(right_solve)
                 advance()
+        if turn == 0:
+            for piece in grad_pieces:
+                piece.start(0)
         if 0 <= turn - LAG < steps:
             attend(grad_pieces, turn - LAG)
             advance()

time: 47.8 us -> 46.8 us (0.979)
  Pallas kernels: 45.3 us -> 44.3 us
    pallas_call x1, Pallas kernels: 45.3 us -> 44.3 us  [per_device(): pl.pallas_call(functools.partial(kernel, dp_count, owners), out_shape=jax...]
where the time goes in v3:
time: 46.8 us; the launch traced here: 46.7 us
  Pallas kernels  44.3 us (95%)
  local copies, waits for them, and re-layouts  1.67 us (4%)
  between operations  0.67 us (1%)
    pallas_call x1, Pallas kernels, per_device(): pl.pallas_call(functools.partial(kernel, dp_count, owners), out_shape=jax...  44.3 us
    unnamed x3, local copies, waits for them, and re-layouts  1.67 us

profile of v3, /device:TPU:0, one launch (start us, length us, event | category | flops | bytes accessed | tf_op | source)
XLA Modules:
  0.0 46.7 jit_solution(1166262417874501117)
XLA Ops:
  0.7 0.0 copy-start
  0.7 1.0 %copy-done = bf16[1,1,512,512]{3,2,1,0:T(8,128)(2,1)S(1)} copy-done((bf16[1,1,512,512]{3,2,1,0:T(8,128)(2,1)S(1)}, bf16[1,1,512,512]{3,2,1,0:T(8,128)(2,1)}, u32[]{:S(2)}) %copy-start) | copy-done | bytes 524312
  1.7 44.3 %shard_map.28 = bf16[64,512]{1,0:T(8,128)(2,1)S(1)} custom-call(s32[1]{0:T(128)S(6)} %copy.4.layer_ref, bf16[512,512]{1,0:T(8,128)(2,1)S(1)} %bitcast.2), custom_call_target="tpu_custom_call" | custom-call | tf_op jit(solution)/shard_map/pallas_call | solution.py:272
  46.0 0.6 %copy.5 = bf16[1,64,512]{2,1,0:T(8,128)(2,1)} copy(bf16[1,64,512]{2,1,0:T(8,128)(2,1)S(1)} %bitcast.3) | data formatting | bytes 131072
Async XLA Ops:
  0.7 1.0 %copy-start = (bf16[1,1,512,512]{3,2,1,0:T(8,128)(2,1)S(1)}, bf16[1,1,512,512]{3,2,1,0:T(8,128)(2,1)}, u32[]{:S(2)}) copy-start(bf16[1,1,512,512]{3,2,1,0:T(8,128)(2,1)} %param.2) | copy-start | bytes 1572868
